TPU v7x, 32 devices: a whole 2x2x4 slice. The times are simulated.
32 devices in a mesh: dp: 4 (over x, core), expert: 8 (over z, y).
Axes of the slice: x: 2, y: 2, z: 4, core: 2. Of those that a mesh axis runs over, the one named last changes fastest.
Arguments:
- tokens: bfloat16 [5120, 131072], P(None, ('dp', 'expert')), may hold values from -24 to 24, as said below
- router: bfloat16 [5120, 40], P(None, 'expert'), may hold values from -1 to 1, as said below
- device_pick: int32 [3, 131072], P(None, 'dp'), may hold values from 0 to 7, as said below
- expert_pick: int32 [6, 131072], P(None, 'dp'), may hold values from 0 to 39, as said below
Outputs:
- gates: float32 [6, 131072], P(None, 'dp')
- device_max: float32 [8, 131072], P('expert', 'dp')
- balance: float32 [3], replicated
Inputs may be any that keep to these rules, and one draw needn't show every extreme that they name: tokens lie within the range; in each column the values are of order one, except in a few columns. router entries are of order 1 / sqrt(5120). `device_pick`: each column names 3 different devices. `expert_pick`: each column names 6 different experts, two on each device of the column's device_pick, in that order; the device of expert e is e // 5.
All inputs are finite; a program needn't handle non-finite values.
Results may differ from a plain program's by a relative error of at most 0.0003.
Values may be sent and summed in bfloat16 or wider, within the bound.
A program may use at most 128 MiB of HBM per device.

v0:
```python
import jax
import jax.numpy as jnp
from jax import lax
from jax.sharding import PartitionSpec as P

TOP = 6
DEV_TOP = 3


def local(tokens, router, device_pick, expert_pick):
    share = tokens.shape[1]
    num_devices = lax.axis_size("expert")
    per_device = router.shape[1]
    num_experts = per_device * num_devices
    tok_rows = share * num_devices
    my_index = lax.axis_index("expert")
    total_tokens = tok_rows * lax.axis_size("dp")
    scores = jnp.dot(
        tokens.T,
        lax.all_gather(router, "expert", axis=1, tiled=True),
        preferred_element_type=jnp.float32,
    ).T
    peak = jnp.max(scores, axis=0, keepdims=True)
    raised = jnp.exp(scores - peak)
    probs = raised / jnp.sum(raised, axis=0, keepdims=True)
    first_col = my_index * share
    experts_here = lax.dynamic_slice_in_dim(expert_pick, first_col, share, 1)
    devices_here = lax.dynamic_slice_in_dim(device_pick, first_col, share, 1)
    col_gates = jnp.take_along_axis(probs, experts_here, axis=0)
    col_maxima = jnp.max(probs.reshape(num_devices, per_device, share), axis=1)
    gates = lax.all_gather(col_gates, "expert", axis=1, tiled=True)
    device_max = lax.all_to_all(col_maxima, "expert", split_axis=0, concat_axis=1, tiled=True)
    prob_sum = jnp.sum(probs, axis=1)
    all_ids = jnp.arange(num_experts, dtype=jnp.int32)
    counts = jnp.sum(
        (all_ids[:, None, None] == experts_here[None, :, :]).astype(jnp.float32), axis=(1, 2)
    )
    dev_ids = jnp.arange(num_devices, dtype=jnp.int32)
    sent_counts = jnp.sum(
        (dev_ids[:, None, None] == devices_here[None, :, :]).astype(jnp.float32), axis=(1, 2)
    )
    prob_sum, counts, sent_counts = lax.psum((prob_sum, counts, sent_counts), ("dp", "expert"))
    freq = counts * (num_experts / (TOP * total_tokens))
    prob = prob_sum / total_tokens
    dev_freq = jnp.mean(freq.reshape(num_devices, per_device), axis=1)
    dev_prob = jnp.sum(prob.reshape(num_devices, per_device), axis=1)
    sent = sent_counts * (num_devices / (DEV_TOP * total_tokens))
    balance = jnp.stack(
        [jnp.sum(freq * prob), jnp.sum(dev_freq * dev_prob), jnp.sum(sent * dev_prob)]
    )
    return (gates, device_max, balance)


def solution(mesh):
    placed = (P(None, ("dp", "expert")), P(None, "expert"), P(None, "dp"), P(None, "dp"))
    return jax.shard_map(
        local,
        mesh=mesh,
        in_specs=placed,
        out_specs=(P(None, "dp"), P("expert", "dp"), P()),
        check_vma=False,
    )
```

profile of v0, /device:TPU:0, one launch (start us, length us, event | category | flops | bytes accessed | tf_op | source)
XLA Modules:
  0.0 334.4 jit_solution(717634554727108604)
XLA Ops:
  0.6 0.0 copy-start
  0.6 33.8 %all-gather = bf16[8,5,5120]{2,1,0:T(8,128)(2,1)S(1)} all-gather(bf16[1,5,5120]{2,1,0:T(8,128)(2,1)} %bitcast.14), channel_id=1, replica_groups=mesh['dp'=4,'expert'=8] {'expert'}, dimensions={0}, use_global_device_ids=true | all-gather | bytes 460800 | tf_op jit(solution)/shard_map/all_gather | solution.py:20
  34.4 0.2 reshape.50
  34.6 16.7 %fusion.4 = (f32[4096]{0:T(1024)S(1)}, f32[40,4096]{1,0:T(8,128)S(1)}) fusion(bf16[40,5120]{1,0:T(8,128)(2,1)S(1)} %reshape.50, bf16[5120,4096]{1,0:T(8,128)(2,1)} %param.4), kind=kOutput, calls=%fused_computation.20 | convolution fusion | flops 1677881344 | bytes 43024384 | tf_op jit(solution)/shard_map/dot_general | solution.py:18
  51.3 0.1 fusion.1
  51.4 0.2 fusion.2
  51.6 0.1 reshape.35
  51.8 0.3 reduce_max.19
  52.1 0.8 all_to_all.12
  52.8 5.6 %all-to-all-start = ((f32[8,1,4096]{2,1,0:T(1,128)}), f32[8,1,4096]{2,1,0:T(1,128)S(1)}, u32[]{:S(2)}, u32[]{:S(2)}) async-start(f32[8,1,4096]{2,1,0:T(1,128)} %all_to_all.12), calls=%async_computation | async-start | bytes 262144 | tf_op jit(solution)/shard_map/all_to_all | solution.py:32
  58.5 0.0 copy-done
  58.5 0.2 convert_reduce_fusion.1
  58.7 1.0 bitcast_or_fusion
  59.7 0.1 reshape.38
  59.7 0.5 convert_reduce_fusion
  60.2 195.6 %gather_fusion = f32[24576]{0:T(1024)S(1)} fusion(f32[40,4096]{1,0:T(8,128)S(1)} %get-tuple-element.9, s32[24576]{0:T(1024)S(1)} %reshape.38), kind=kCustom, calls=%fused_computation | custom fusion | bytes 393216 | tf_op jit(solution)/shard_map/jit(take_along_axis)/gather | solution.py:29
  255.8 32.8 %all_gather.7 = f32[6,32768]{1,0:T(8,128)S(1)} all-gather(f32[6,4096]{1,0:T(8,128)S(1)} %and_select_fusion), channel_id=1, replica_groups=mesh['dp'=4,'expert'=8] {'expert'}, dimensions={1}, use_global_device_ids=true | all-gather | bytes 884736 | tf_op jit(solution)/shard_map/all_gather | solution.py:31
  288.6 39.9 %all-reduce = (f32[40]{0:T(128)S(1)}, f32[40]{0:T(128)S(1)}, f32[8]{0:T(128)S(1)}) all-reduce(f32[40]{0:T(128)S(1)} %get-tuple-element.8, f32[40]{0:T(128)S(1)} %convert_reduce_fusion, f32[8]{0:T(128)S(1)} %convert_reduce_fusion.1), channel_id=1, replica_groups=mesh['dp'=4,'expert'=8] {'dp','expert'}, use_global_device_ids=true, to_apply=%region_6.7 | all-reduce | flops 88 | bytes 704 | tf_op jit(solution)/shard_map/psum | solution.py:42
  328.6 0.6 multiply_reduce_fusion.2
  329.2 0.1 reshape.37
  329.2 0.1 reshape.36
  329.3 0.1 reduce_sum.86
  329.4 0.1 reduce_sum.85
  329.6 0.7 multiply_reduce_fusion.1
  330.2 2.5 pad_maximum_fusion
  332.7 0.0 all-to-all-done
  332.7 1.0 copy.9
  333.7 0.7 copy.10
  (3 shorter events, 0.1 us)
Async XLA Ops:
  0.6 57.8 %copy-start = (s32[3,32768]{1,0:T(4,128)S(1)}, s32[3,32768]{1,0:T(4,128)}, u32[]{:S(2)}) copy-start(s32[3,32768]{1,0:T(4,128)} %param.6) | copy-start | bytes 1179652
  52.8 279.9 %all-to-all-start = ((f32[8,1,4096]{2,1,0:T(1,128)}), f32[8,1,4096]{2,1,0:T(1,128)S(1)}, u32[]{:S(2)}, u32[]{:S(2)}) async-start(f32[8,1,4096]{2,1,0:T(1,128)} %all_to_all.12), calls=%async_computation | async-start | bytes 262144 | tf_op jit(solution)/shard_map/all_to_all | solution.py:32
where the time goes:
time: 335 us; the launch traced here: 334 us
  local copies, waits for them, and re-layouts  198 us (59%)
  blocking collectives  106 us (32%)
  matrix products  16.7 us (5%)
  other arithmetic  6.37 us (2%)
  starting transfers between devices  5.62 us (2%)
    gather x3, local copies, waits for them, and re-layouts, local(): col_gates = jnp.take_along_axis(probs, experts_here, axis=0)  196 us
    psum x1, blocking collectives, local(): lax.psum((prob_sum, counts, sent_counts), ('dp', 'expert'))  39.9 us
    all_gather x1, blocking collectives, local(): lax.all_gather(router, 'expert', axis=1, tiled=True)  33.8 us
    all_gather x1, blocking collectives, local(): gates = lax.all_gather(col_gates, 'expert', axis=1, tiled=True)  32.8 us
    dot_general x1, matrix products, local(): jnp.dot(tokens.T, lax.all_gather(router, 'expert', axis=1, tiled=True), p...  16.7 us
  transfers between devices with their start and end apart: 1, of which 0 were waited for; matrix products, arithmetic and copies ran while one was open for 60% of the time, Pallas kernels for 0%

commit v1 on v0

v1 whole, which is shorter than its diff:
```python
import functools

import jax
import jax.numpy as jnp
from jax import lax
from jax.experimental import pallas as pl
from jax.experimental.pallas import tpu as pltpu
from jax.sharding import PartitionSpec as P

MESH = pl.DeviceIdType.MESH
TOP = 6
DEV_TOP = 3
SLOT = 8
LOG2E = 1.4426950408889634
GATE_SCALE = 2048.0
MAX_SCALE = 1048576.0
NEG = -1e30


def kernel(
    sizes, tokens, router, device_pick, expert_pick,
    gates, device_max, balance,
    tok, rows, picks, dpicks, sent_msg, recv_msg, cnt_msg, cnt_recv, bal_msg, bal_recv, prob_acc,
    tok_sem, pick_sem, rs_sem, rr_sem, ps_sem, pr_sem, ms_sem, mr_sem, cs_sem, cr_sem, bs_sem, br_sem,
):
    ndp, ndev, per_dev, width, chunks = sizes
    depth = tokens.shape[0]
    share = tokens.shape[1]
    total = share * ndev * ndp
    nrows = ndev * SLOT
    everyone = ndp * ndev
    half = depth // 2
    dp, me = lax.axis_index("dp"), lax.axis_index("expert")
    lin = dp * ndev + me
    core = lax.rem(dp, 2)
    partner = dp + 1 - 2 * core

    def token_copy(c):
        return pltpu.make_async_copy(
            tokens.at[:, pl.ds(pl.multiple_of(c * width, width), width)], tok.at[c], tok_sem.at[c]
        )

    mine = pl.ds(pl.multiple_of(me * share, share), share)
    pick_copy = pltpu.make_async_copy(expert_pick.at[:, mine], picks, pick_sem.at[0])
    dpick_copy = pltpu.make_async_copy(device_pick.at[:, mine], dpicks, pick_sem.at[1])
    pick_copy.start()
    dpick_copy.start()
    for c in range(chunks):
        token_copy(c).start()

    barrier = pltpu.get_barrier_semaphore()

    def other(j):
        t = lax.rem(lin + j, everyone)
        return (t // ndev, lax.rem(t, ndev))

    def greet(j, carry):
        pl.semaphore_signal(barrier, inc=1, device_id=other(j), device_id_type=MESH)
        return carry

    lax.fori_loop(1, everyone, greet, 0)
    pl.semaphore_wait(barrier, everyone - 1)

    my_half = pl.ds(pl.multiple_of(core * half, half), half)
    other_half = pl.ds(pl.multiple_of((1 - core) * half, half), half)
    my_rows = pl.ds(pl.multiple_of(me * SLOT, SLOT), SLOT)

    def router_copy(j):
        peer = lax.rem(me + j, ndev)
        return pltpu.make_async_remote_copy(
            src_ref=router.at[:, my_half], dst_ref=rows.at[my_rows, my_half],
            send_sem=rs_sem.at[j], recv_sem=rr_sem.at[j], device_id=(dp, peer), device_id_type=MESH,
        )

    def partner_copy(j):
        src = lax.rem(me + ndev - j, ndev)
        block = rows.at[pl.ds(pl.multiple_of(src * SLOT, SLOT), SLOT), my_half]
        return pltpu.make_async_remote_copy(
            src_ref=block, dst_ref=block, send_sem=ps_sem.at[j], recv_sem=pr_sem.at[j],
            device_id=(partner, me), device_id_type=MESH,
        )

    for j in range(1, ndev):
        router_copy(j).start()
    own = pltpu.make_async_copy(router, rows.at[my_rows, :], rs_sem.at[0])
    own.start()

    pick_copy.wait()
    dpick_copy.wait()
    row = lax.broadcasted_iota(jnp.int32, (nrows, 128), 0)
    lane = lax.broadcasted_iota(jnp.int32, (nrows, 128), 1)
    one, nil = jnp.float32(1.0), jnp.float32(0.0)
    ids = (row // SLOT) * per_dev + lax.rem(row, SLOT)
    ids = jnp.where(lax.rem(row, SLOT) < per_dev, ids, -1)
    dev_ids = jnp.where(lax.rem(row, SLOT) == 0, row // SLOT, -1)

    def count(i, carry):
        counts, sends = carry
        cols = pl.ds(pl.multiple_of(i * 128, 128), 128)
        for k in range(TOP):
            counts = counts + jnp.where(picks[k : k + 1, cols] == ids, one, nil)
        for k in range(DEV_TOP):
            sends = sends + jnp.where(dpicks[k : k + 1, cols] == dev_ids, one, nil)
        return counts, sends

    zero = jnp.zeros((nrows, 128), jnp.float32)
    counts, sends = lax.fori_loop(0, share // 128, count, (zero, zero))
    counts = jnp.sum(counts, axis=1, keepdims=True)
    sends = jnp.sum(sends, axis=1, keepdims=True)
    pages = cnt_msg.shape[1] // 2 // 128
    for p in range(pages):
        spot = row == lane + p * 128
        cnt_msg[:, p * 128 : (p + 1) * 128] = jnp.sum(jnp.where(spot, counts, nil), axis=0, keepdims=True)
        cnt_msg[:, (pages + p) * 128 : (pages + p + 1) * 128] = jnp.sum(
            jnp.where(spot, sends, nil), axis=0, keepdims=True
        )
    cnt_recv[lin] = cnt_msg[...]

    def count_copy(j):
        return pltpu.make_async_remote_copy(
            src_ref=cnt_msg, dst_ref=cnt_recv.at[lin], send_sem=cs_sem, recv_sem=cr_sem,
            device_id=other(j), device_id_type=MESH,
        )

    def start_count(j, carry):
        count_copy(j).start()
        return carry

    lax.fori_loop(1, everyone, start_count, 0)

    own.wait()
    for j in range(1, ndev):
        router_copy(j).wait_recv()
        partner_copy(j).start()
    for j in range(1, ndev):
        partner_copy(j).wait_recv()

    prob_acc[...] = zero
    wide_row = lax.broadcasted_iota(jnp.int32, (nrows, width), 0)
    wide_ids = (wide_row // SLOT) * per_dev + lax.rem(wide_row, SLOT)
    real = lax.rem(wide_row, SLOT) < per_dev
    wide_ids = jnp.where(real, wide_ids, -1)
    msg_row = lax.broadcasted_iota(jnp.int32, (4, width), 0)

    def message_copy(j, c):
        peer = lax.rem(me + j, ndev)
        return pltpu.make_async_remote_copy(
            src_ref=sent_msg.at[peer, c], dst_ref=recv_msg.at[me, c],
            send_sem=ms_sem.at[j], recv_sem=mr_sem.at[j], device_id=(dp, peer), device_id_type=MESH,
        )

    def step(c, carry):
        token_copy(c).wait()
        scores = jnp.dot(rows[...], tok[c], preferred_element_type=jnp.float32)
        scores = jnp.where(real, scores, NEG)
        peak = jnp.max(scores, axis=0, keepdims=True)
        shifted = scores - peak
        raised = jnp.exp(shifted)
        norm = jnp.sum(raised, axis=0, keepdims=True)
        probs = raised * (1.0 / norm)
        acc = prob_acc[...]
        for i in range(width // 128):
            acc = acc + probs[:, i * 128 : (i + 1) * 128]
        prob_acc[...] = acc
        log_norm = jnp.log(norm)
        cols = pl.ds(pl.multiple_of(c * width, width), width)
        codes = []
        for k in range(TOP):
            hit = picks[k : k + 1, cols] == wide_ids
            picked = jnp.sum(jnp.where(hit, shifted, nil), axis=0, keepdims=True)
            code = (log_norm - picked) * (LOG2E * GATE_SCALE) + 0.5
            codes.append(jnp.clip(code, 0.0, 65535.0).astype(jnp.int32))
        words = [codes[k] + jnp.left_shift(codes[k + TOP // 2], 16) for k in range(TOP // 2)]
        base = jnp.where(msg_row == 0, words[0], jnp.where(msg_row == 1, words[1], words[2]))
        for d in range(ndev):
            best = jnp.max(shifted[d * SLOT : (d + 1) * SLOT, :], axis=0, keepdims=True)
            code = (log_norm - best) * (LOG2E * MAX_SCALE) + 0.5
            code = jnp.clip(code, 0.0, 2.0e9).astype(jnp.int32)
            sent_msg[d, c] = jnp.where(msg_row == 3, code, base)
        recv_msg[me, c] = sent_msg[me, c]
        for j in range(1, ndev):
            message_copy(j, c).start()
        return carry

    lax.fori_loop(0, chunks, step, 0)

    pltpu.make_async_copy(cnt_recv.at[pl.ds(0, everyone - 1)], cnt_recv.at[pl.ds(0, everyone - 1)], cr_sem).wait()
    all_counts = jnp.sum(cnt_recv[...], axis=0)
    freq = jnp.zeros((nrows, 1), jnp.float32)
    dev_freq = jnp.zeros((nrows, 1), jnp.float32)
    sent = jnp.zeros((nrows, 1), jnp.float32)
    for p in range(pages):
        here = all_counts[:, p * 128 : (p + 1) * 128]
        there = all_counts[:, (pages + p) * 128 : (pages + p + 1) * 128]
        where = lane + p * 128
        same = (where // SLOT) == (row // SLOT)
        freq = freq + jnp.sum(jnp.where(where == row, here, nil), axis=1, keepdims=True)
        dev_freq = dev_freq + jnp.sum(jnp.where(same, here, nil), axis=1, keepdims=True)
        sent = sent + jnp.sum(jnp.where(same, there, nil), axis=1, keepdims=True)
    experts = ndev * per_dev
    freq = freq * (experts / (TOP * total))
    dev_freq = dev_freq * (experts / (TOP * total) / per_dev)
    sent = sent * (ndev / (DEV_TOP * total))
    prob = prob_acc[...] * (1.0 / total)
    one_lane = lax.broadcasted_iota(jnp.int32, (1, 128), 1)
    result = jnp.zeros((1, 128), jnp.float32)
    for i, factor in enumerate((freq, dev_freq, sent)):
        part = jnp.sum(jnp.sum(prob * factor, axis=0, keepdims=True), axis=1, keepdims=True)
        result = jnp.where(one_lane == i, part, result)
    bal_msg[...] = result
    bal_recv[lin] = result

    def bal_copy(j):
        return pltpu.make_async_remote_copy(
            src_ref=bal_msg, dst_ref=bal_recv.at[lin], send_sem=bs_sem, recv_sem=br_sem,
            device_id=other(j), device_id_type=MESH,
        )

    def start_bal(j, carry):
        bal_copy(j).start()
        return carry

    lax.fori_loop(1, everyone, start_bal, 0)

    def decode(src):
        def body(c, carry):
            words = recv_msg[src, c]
            low = jnp.exp2((words & 65535).astype(jnp.float32) * (-1.0 / GATE_SCALE))
            high = jnp.exp2(lax.shift_right_logical(words, 16).astype(jnp.float32) * (-1.0 / GATE_SCALE))
            top = jnp.exp2(words[3:4, :].astype(jnp.float32) * (-1.0 / MAX_SCALE))
            cols = pl.ds(pl.multiple_of(src * share + c * width, width), width)
            gates[0:3, cols] = low[0:3]
            gates[3:6, cols] = high[0:3]
            device_max[:, cols] = top
            return carry

        lax.fori_loop(0, chunks, body, 0)

    decode(me)
    for j in range(1, ndev):
        src = lax.rem(me + ndev - j, ndev)
        pltpu.make_async_copy(recv_msg.at[src], recv_msg.at[src], mr_sem.at[j]).wait()
        decode(src)

    pltpu.make_async_copy(bal_recv.at[pl.ds(0, everyone - 1)], bal_recv.at[pl.ds(0, everyone - 1)], br_sem).wait()
    sums = jnp.sum(bal_recv[...], axis=0)
    for i in range(3):
        balance[i] = jnp.sum(jnp.where(one_lane == i, sums, nil))

    for j in range(1, ndev):
        router_copy(j).wait_send()
        partner_copy(j).wait_send()
        peer = lax.rem(me + j, ndev)
        pltpu.make_async_copy(sent_msg.at[peer], sent_msg.at[peer], ms_sem.at[j]).wait()
    pltpu.make_async_copy(cnt_recv.at[pl.ds(0, everyone - 1)], cnt_recv.at[pl.ds(0, everyone - 1)], cs_sem).wait()
    pltpu.make_async_copy(bal_recv.at[pl.ds(0, everyone - 1)], bal_recv.at[pl.ds(0, everyone - 1)], bs_sem).wait()


def local(tokens, router, device_pick, expert_pick):
    depth, share = tokens.shape
    ndev, ndp = lax.axis_size("expert"), lax.axis_size("dp")
    per_dev = router.shape[1]
    width = min(512, share)
    chunks = share // width
    nrows = ndev * SLOT
    padded = (nrows + 127) // 128 * 128
    everyone = ndp * ndev
    router = jnp.pad(router.T, ((0, SLOT - per_dev), (0, 0)))
    dma = pltpu.SemaphoreType.DMA
    gates, device_max, balance = pl.pallas_call(
        functools.partial(kernel, (ndp, ndev, per_dev, width, chunks)),
        out_shape=(
            jax.ShapeDtypeStruct((TOP, share * ndev), jnp.float32),
            jax.ShapeDtypeStruct((1, share * ndev), jnp.float32),
            jax.ShapeDtypeStruct((3,), jnp.float32),
        ),
        in_specs=[
            pl.BlockSpec(memory_space=pl.ANY),
            pl.BlockSpec(memory_space=pltpu.VMEM),
            pl.BlockSpec(memory_space=pl.ANY),
            pl.BlockSpec(memory_space=pl.ANY),
        ],
        out_specs=(
            pl.BlockSpec(memory_space=pltpu.VMEM),
            pl.BlockSpec(memory_space=pltpu.VMEM),
            pl.BlockSpec(memory_space=pltpu.SMEM),
        ),
        scratch_shapes=[
            pltpu.VMEM((chunks, depth, width), jnp.bfloat16),
            pltpu.VMEM((nrows, depth), jnp.bfloat16),
            pltpu.VMEM((TOP, share), jnp.int32),
            pltpu.VMEM((DEV_TOP, share), jnp.int32),
            pltpu.VMEM((ndev, chunks, 4, width), jnp.int32),
            pltpu.VMEM((ndev, chunks, 4, width), jnp.int32),
            pltpu.VMEM((1, 2 * padded), jnp.float32),
            pltpu.VMEM((everyone, 1, 2 * padded), jnp.float32),
            pltpu.VMEM((1, 128), jnp.float32),
            pltpu.VMEM((everyone, 1, 128), jnp.float32),
            pltpu.VMEM((nrows, 128), jnp.float32),
            dma((chunks,)),
            dma((2,)),
            dma((ndev,)),
            dma((ndev,)),
            dma((ndev,)),
            dma((ndev,)),
            dma((ndev,)),
            dma((ndev,)),
            dma,
            dma,
            dma,
            dma,
        ],
        compiler_params=pltpu.CompilerParams(
            collective_id=0, has_side_effects=True, vmem_limit_bytes=60 * 1024 * 1024
        ),
        name="route",
    )(tokens, router, device_pick, expert_pick)
    return gates, device_max, balance


def solution(mesh):
    placed = (P(None, ("dp", "expert")), P(None, "expert"), P(None, "dp"), P(None, "dp"))
    return jax.shard_map(
        local,
        mesh=mesh,
        in_specs=placed,
        out_specs=(P(None, "dp"), P("expert", "dp"), P()),
        check_vma=False,
    )
```

time: 335 us -> 44.7 us (0.13)
  local copies, waits for them, and re-layouts: 198 us -> 6.5 us
  blocking collectives: 106 us -> 0 us
  Pallas kernels: 0 us -> 37.3 us
  matrix products: 16.7 us -> 0 us
  other arithmetic: 6.37 us -> 0 us
  starting transfers between devices: 5.62 us -> 0 us
    gather x3 -> x0, local copies, waits for them, and re-layouts: 196 us -> none  [local(): col_gates = jnp.take_along_axis(probs, experts_here, axis=0)]
    all_gather x2 -> x0, blocking collectives: 66.6 us -> none  [the longest x1 33.8 us: local(): lax.all_gather(router, 'expert', axis=1, tiled=True)]
    psum x1 -> x0, blocking collectives: 39.9 us -> none  [local(): lax.psum((prob_sum, counts, sent_counts), ('dp', 'expert'))]
    pallas_call x0 -> x1, Pallas kernels: none -> 37.3 us  [local(): pl.pallas_call(functools.partial(kernel, (ndp, ndev, per_dev, width, chun...]
    dot_general x1 -> x0, matrix products: 16.7 us -> none  [local(): jnp.dot(tokens.T, lax.all_gather(router, 'expert', axis=1, tiled=True), p...]
    all_to_all x1 -> x0, starting transfers between devices: 5.62 us -> none  [local(): lax.all_to_all(col_maxima, 'expert', split_axis=0, concat_axis=1, tiled=T...]
  transfers between devices with their start and end apart: 1 -> 0, of which waited for: 0 -> 0; matrix products, arithmetic and copies ran while one was open for 60% -> 0% of each run, Pallas kernels for 0% -> 0%
where the time goes in v1:
time: 44.7 us; the launch traced here: 44.5 us
  Pallas kernels  37.3 us (83%)
  local copies, waits for them, and re-layouts  6.5 us (15%)
  between operations  0.64 us (1%)
    pallas_call x1, Pallas kernels, local(): pl.pallas_call(functools.partial(kernel, (ndp, ndev, per_dev, width, chun...  37.3 us
    unnamed x3, local copies, waits for them, and re-layouts  4.96 us
    pad x1, local copies, waits for them, and re-layouts, local(): router = jnp.pad(router.T, ((0, SLOT - per_dev), (0, 0)))  1.54 us

profile of v1, /device:TPU:0, one launch (start us, length us, event | category | flops | bytes accessed | tf_op | source)
XLA Modules:
  0.0 44.5 jit_solution(7118912070222347140)
XLA Ops:
  0.6 1.5 %pad.4.router = bf16[8,5120]{1,0:T(8,128)(2,1)} pad(bf16[5,5120]{1,0:T(8,128)(2,1)} %bitcast.1, bf16[]{:T(256)} %constant.2.clone.1), padding=0_3x0_0 | pad | bytes 133122 | tf_op jit(solution)/shard_map/jit(_pad)/pad | solution.py:268
  2.2 37.3 %route.1 = (f32[6,32768]{1,0:T(8,128)}, f32[1,32768]{1,0:T(1,128)}, f32[3]{0:T(128)}) custom-call(bf16[5120,4096]{1,0:T(8,128)(2,1)} %tokens.1, bf16[8,5120]{1,0:T(8,128)(2,1)} %pad.4.router, s32[3,32768]{1,0:T(4,128)} %device_pick.1, s32[6,32768]{1,0:T(8,128)} %expert_pick.1), custom_call_target="tpu_custom_call" | custom-call | tf_op jit(solution)/shard_map/route/pallas_call | solution.py:270
  39.5 2.3 %copy.10 = f32[6,32768]{1,0:T(8,128)} copy(f32[6,32768]{1,0:T(8,128)} %get-tuple-element.6) | data formatting | bytes 1572864
  41.8 1.6 %copy.11 = f32[1,32768]{1,0:T(1,128)} copy(f32[1,32768]{1,0:T(1,128)} %get-tuple-element.7) | data formatting | bytes 262144
  43.3 1.1 %copy.12 = f32[3]{0:T(128)} copy(f32[3]{0:T(128)} %get-tuple-element.8) | data formatting | bytes 24

commit v2 on v1

--- a/solution.py
+++ b/solution.py
@@ -13,15 +13,16 @@
 SLOT = 8
 LOG2E = 1.4426950408889634
 GATE_SCALE = 2048.0
-MAX_SCALE = 1048576.0
 NEG = -1e30
+VMEM = 67043328
 
 
 def kernel(
     sizes, tokens, router, device_pick, expert_pick,
-    gates, device_max, balance,
-    tok, rows, picks, dpicks, sent_msg, recv_msg, cnt_msg, cnt_recv, bal_msg, bal_recv, prob_acc,
-    tok_sem, pick_sem, rs_sem, rr_sem, ps_sem, pr_sem, ms_sem, mr_sem, cs_sem, cr_sem, bs_sem, br_sem,
+    recv_msg, balance,
+    tok, raw, own_rows, rows, picks, dpicks, sent_msg, cnt_msg, cnt_recv, bal_msg, bal_recv, prob_acc,
+    tok_sem, pick_sem, rs_sem, rr_sem, ys_sem, yr_sem, ps_sem, pr_sem,
+    ms_sem, mr_sem, fs_sem, fr_sem, cs_sem, cr_sem, bs_sem, br_sem,
 ):
     ndp, ndev, per_dev, width, chunks = sizes
     depth = tokens.shape[0]
@@ -43,6 +44,8 @@
     mine = pl.ds(pl.multiple_of(me * share, share), share)
     pick_copy = pltpu.make_async_copy(expert_pick.at[:, mine], picks, pick_sem.at[0])
     dpick_copy = pltpu.make_async_copy(device_pick.at[:, mine], dpicks, pick_sem.at[1])
+    raw_copy = pltpu.make_async_copy(router, raw, pick_sem.at[2])
+    raw_copy.start()
     pick_copy.start()
     dpick_copy.start()
     for c in range(chunks):
@@ -59,30 +62,51 @@
         return carry
 
     lax.fori_loop(1, everyone, greet, 0)
+    raw_copy.wait()
+    pad = jnp.zeros((SLOT - per_dev, depth), jnp.float32)
+    own_rows[...] = jnp.concatenate([raw[...].astype(jnp.float32), pad], axis=0).astype(jnp.bfloat16)
     pl.semaphore_wait(barrier, everyone - 1)
 
+    pairs = ndev // 2
+    my_pair, side = me // 2, lax.rem(me, 2)
+    mate = me + 1 - 2 * side
+
+    def ahead(j):
+        return lax.rem(my_pair + j, pairs) * 2 + side
+
+    def behind(j, which):
+        return lax.rem(my_pair + pairs - j, pairs) * 2 + which
+
     my_half = pl.ds(pl.multiple_of(core * half, half), half)
-    other_half = pl.ds(pl.multiple_of((1 - core) * half, half), half)
     my_rows = pl.ds(pl.multiple_of(me * SLOT, SLOT), SLOT)
 
+    def slot(src):
+        return rows.at[pl.ds(pl.multiple_of(src * SLOT, SLOT), SLOT), my_half]
+
     def router_copy(j):
-        peer = lax.rem(me + j, ndev)
-        return pltpu.make_async_remote_copy(
-            src_ref=router.at[:, my_half], dst_ref=rows.at[my_rows, my_half],
-            send_sem=rs_sem.at[j], recv_sem=rr_sem.at[j], device_id=(dp, peer), device_id_type=MESH,
-        )
-
-    def partner_copy(j):
-        src = lax.rem(me + ndev - j, ndev)
-        block = rows.at[pl.ds(pl.multiple_of(src * SLOT, SLOT), SLOT), my_half]
-        return pltpu.make_async_remote_copy(
-            src_ref=block, dst_ref=block, send_sem=ps_sem.at[j], recv_sem=pr_sem.at[j],
+        return pltpu.make_async_remote_copy(
+            src_ref=own_rows.at[:, my_half], dst_ref=slot(me),
+            send_sem=rs_sem.at[j], recv_sem=rr_sem.at[j], device_id=(dp, ahead(j)), device_id_type=MESH,
+        )
+
+    def mate_copy(j):
+        return pltpu.make_async_remote_copy(
+            src_ref=own_rows.at[:, my_half] if j == 0 else slot(behind(j, side)), dst_ref=slot(behind(j, side)),
+            send_sem=ys_sem.at[j], recv_sem=yr_sem.at[j], device_id=(dp, mate), device_id_type=MESH,
+        )
+
+    def partner_copy(j, other_side):
+        block = slot(behind(j, 1 - side if other_side else side))
+        spot = j + other_side * pairs
+        return pltpu.make_async_remote_copy(
+            src_ref=block, dst_ref=block, send_sem=ps_sem.at[spot], recv_sem=pr_sem.at[spot],
             device_id=(partner, me), device_id_type=MESH,
         )
 
-    for j in range(1, ndev):
+    for j in range(1, pairs):
         router_copy(j).start()
-    own = pltpu.make_async_copy(router, rows.at[my_rows, :], rs_sem.at[0])
+    mate_copy(0).start()
+    own = pltpu.make_async_copy(own_rows, rows.at[my_rows, :], rs_sem.at[0])
     own.start()
 
     pick_copy.wait()
@@ -129,11 +153,17 @@
     lax.fori_loop(1, everyone, start_count, 0)
 
     own.wait()
-    for j in range(1, ndev):
+    for j in range(1, pairs):
         router_copy(j).wait_recv()
-        partner_copy(j).start()
-    for j in range(1, ndev):
-        partner_copy(j).wait_recv()
+        mate_copy(j).start()
+        partner_copy(j, 0).start()
+    for j in range(pairs):
+        mate_copy(j).wait_recv()
+        partner_copy(j, 1).start()
+    for j in range(1, pairs):
+        partner_copy(j, 0).wait_recv()
+    for j in range(pairs):
+        partner_copy(j, 1).wait_recv()
 
     prob_acc[...] = zero
     wide_row = lax.broadcasted_iota(jnp.int32, (nrows, width), 0)
@@ -143,11 +173,22 @@
     msg_row = lax.broadcasted_iota(jnp.int32, (4, width), 0)
 
     def message_copy(j, c):
-        peer = lax.rem(me + j, ndev)
-        return pltpu.make_async_remote_copy(
-            src_ref=sent_msg.at[peer, c], dst_ref=recv_msg.at[me, c],
-            send_sem=ms_sem.at[j], recv_sem=mr_sem.at[j], device_id=(dp, peer), device_id_type=MESH,
-        )
+        return pltpu.make_async_remote_copy(
+            src_ref=sent_msg.at[lax.rem(my_pair + j, pairs), c], dst_ref=recv_msg.at[me, c],
+            send_sem=ms_sem.at[j], recv_sem=mr_sem.at[j, c], device_id=(dp, ahead(j)), device_id_type=MESH,
+        )
+
+    def forward_copy(j, c):
+        src = behind(j, side)
+        return pltpu.make_async_remote_copy(
+            src_ref=sent_msg.at[my_pair, c] if j == 0 else recv_msg.at[src, c], dst_ref=recv_msg.at[src, c],
+            send_sem=fs_sem.at[j], recv_sem=fr_sem.at[j], device_id=(dp, mate), device_id_type=MESH,
+        )
+
+    def forward(c):
+        for j in range(1, pairs):
+            message_copy(j, c).wait_recv()
+            forward_copy(j, c).start()
 
     def step(c, carry):
         token_copy(c).wait()
@@ -172,16 +213,26 @@
             codes.append(jnp.clip(code, 0.0, 65535.0).astype(jnp.int32))
         words = [codes[k] + jnp.left_shift(codes[k + TOP // 2], 16) for k in range(TOP // 2)]
         base = jnp.where(msg_row == 0, words[0], jnp.where(msg_row == 1, words[1], words[2]))
+        tops = []
         for d in range(ndev):
             best = jnp.max(shifted[d * SLOT : (d + 1) * SLOT, :], axis=0, keepdims=True)
-            code = (log_norm - best) * (LOG2E * MAX_SCALE) + 0.5
-            code = jnp.clip(code, 0.0, 2.0e9).astype(jnp.int32)
-            sent_msg[d, c] = jnp.where(msg_row == 3, code, base)
-        recv_msg[me, c] = sent_msg[me, c]
-        for j in range(1, ndev):
+            code = (log_norm - best) * (LOG2E * GATE_SCALE) + 0.5
+            tops.append(jnp.clip(code, 0.0, 65535.0).astype(jnp.int32))
+        for p in range(pairs):
+            top = tops[2 * p] + jnp.left_shift(tops[2 * p + 1], 16)
+            sent_msg[p, c] = jnp.where(msg_row == 3, top, base)
+        recv_msg[me, c] = sent_msg[my_pair, c]
+        for j in range(1, pairs):
             message_copy(j, c).start()
+        forward_copy(0, c).start()
+
+        @pl.when(c >= lag)
+        def _():
+            forward(c - lag)
+
         return carry
 
+    lag = min(3, chunks)
     lax.fori_loop(0, chunks, step, 0)
 
     pltpu.make_async_copy(cnt_recv.at[pl.ds(0, everyone - 1)], cnt_recv.at[pl.ds(0, everyone - 1)], cr_sem).wait()
@@ -222,38 +273,54 @@
 
     lax.fori_loop(1, everyone, start_bal, 0)
 
-    def decode(src):
+    for c in range(chunks - lag, chunks):
+        forward(c)
+    for j in range(pairs):
+        src = behind(j, 1 - side)
+        pltpu.make_async_copy(recv_msg.at[src], recv_msg.at[src], fr_sem.at[j]).wait()
+
+    pltpu.make_async_copy(bal_recv.at[pl.ds(0, everyone - 1)], bal_recv.at[pl.ds(0, everyone - 1)], br_sem).wait()
+    balance[...] = jnp.sum(bal_recv[...], axis=0)
+
+    for j in range(pairs):
+        if j:
+            router_copy(j).wait_send()
+            partner_copy(j, 0).wait_send()
+            pltpu.make_async_copy(sent_msg.at[0], sent_msg.at[0], ms_sem.at[j]).wait()
+        mate_copy(j).wait_send()
+        partner_copy(j, 1).wait_send()
+        pltpu.make_async_copy(sent_msg.at[0], sent_msg.at[0], fs_sem.at[j]).wait()
+    pltpu.make_async_copy(cnt_recv.at[pl.ds(0, everyone - 1)], cnt_recv.at[pl.ds(0, everyone - 1)], cs_sem).wait()
+    pltpu.make_async_copy(bal_recv.at[pl.ds(0, everyone - 1)], bal_recv.at[pl.ds(0, everyone - 1)], bs_sem).wait()
+
+
+def decode(sizes, recv_msg, sums, gates, device_max, balance, gate_buf, top_buf, sem):
+    ndev, share, width, chunks = sizes
+    side = lax.rem(lax.axis_index("expert"), 2)
+    copies = []
+    for src in range(ndev):
+        block = pl.ds(src * share, share)
+
         def body(c, carry):
             words = recv_msg[src, c]
             low = jnp.exp2((words & 65535).astype(jnp.float32) * (-1.0 / GATE_SCALE))
             high = jnp.exp2(lax.shift_right_logical(words, 16).astype(jnp.float32) * (-1.0 / GATE_SCALE))
-            top = jnp.exp2(words[3:4, :].astype(jnp.float32) * (-1.0 / MAX_SCALE))
             cols = pl.ds(pl.multiple_of(src * share + c * width, width), width)
-            gates[0:3, cols] = low[0:3]
-            gates[3:6, cols] = high[0:3]
-            device_max[:, cols] = top
+            gate_buf[0:3, cols] = low[0:3]
+            gate_buf[3:6, cols] = high[0:3]
+            top_buf[:, cols] = jnp.where(side == 0, low[3:4], high[3:4])
             return carry
 
         lax.fori_loop(0, chunks, body, 0)
-
-    decode(me)
-    for j in range(1, ndev):
-        src = lax.rem(me + ndev - j, ndev)
-        pltpu.make_async_copy(recv_msg.at[src], recv_msg.at[src], mr_sem.at[j]).wait()
-        decode(src)
-
-    pltpu.make_async_copy(bal_recv.at[pl.ds(0, everyone - 1)], bal_recv.at[pl.ds(0, everyone - 1)], br_sem).wait()
-    sums = jnp.sum(bal_recv[...], axis=0)
+        copies.append(pltpu.make_async_copy(gate_buf.at[:, block], gates.at[:, block], sem.at[0, src]))
+        copies.append(pltpu.make_async_copy(top_buf.at[:, block], device_max.at[:, block], sem.at[1, src]))
+        copies[-2].start()
+        copies[-1].start()
+    lane = lax.broadcasted_iota(jnp.int32, (1, 128), 1)
     for i in range(3):
-        balance[i] = jnp.sum(jnp.where(one_lane == i, sums, nil))
-
-    for j in range(1, ndev):
-        router_copy(j).wait_send()
-        partner_copy(j).wait_send()
-        peer = lax.rem(me + j, ndev)
-        pltpu.make_async_copy(sent_msg.at[peer], sent_msg.at[peer], ms_sem.at[j]).wait()
-    pltpu.make_async_copy(cnt_recv.at[pl.ds(0, everyone - 1)], cnt_recv.at[pl.ds(0, everyone - 1)], cs_sem).wait()
-    pltpu.make_async_copy(bal_recv.at[pl.ds(0, everyone - 1)], bal_recv.at[pl.ds(0, everyone - 1)], bs_sem).wait()
+        balance[i] = jnp.sum(jnp.where(lane == i, sums[...], jnp.float32(0.0)))
+    for copy in copies:
+        copy.wait()
 
 
 def local(tokens, router, device_pick, expert_pick):
@@ -265,56 +332,72 @@
     nrows = ndev * SLOT
     padded = (nrows + 127) // 128 * 128
     everyone = ndp * ndev
-    router = jnp.pad(router.T, ((0, SLOT - per_dev), (0, 0)))
+    pairs = ndev // 2
     dma = pltpu.SemaphoreType.DMA
-    gates, device_max, balance = pl.pallas_call(
+    messages, sums = pl.pallas_call(
         functools.partial(kernel, (ndp, ndev, per_dev, width, chunks)),
         out_shape=(
-            jax.ShapeDtypeStruct((TOP, share * ndev), jnp.float32),
-            jax.ShapeDtypeStruct((1, share * ndev), jnp.float32),
-            jax.ShapeDtypeStruct((3,), jnp.float32),
+            jax.ShapeDtypeStruct((ndev, chunks, 4, width), jnp.int32),
+            jax.ShapeDtypeStruct((1, 128), jnp.float32),
         ),
-        in_specs=[
-            pl.BlockSpec(memory_space=pl.ANY),
-            pl.BlockSpec(memory_space=pltpu.VMEM),
-            pl.BlockSpec(memory_space=pl.ANY),
-            pl.BlockSpec(memory_space=pl.ANY),
-        ],
-        out_specs=(
-            pl.BlockSpec(memory_space=pltpu.VMEM),
-            pl.BlockSpec(memory_space=pltpu.VMEM),
-            pl.BlockSpec(memory_space=pltpu.SMEM),
-        ),
+        in_specs=[pl.BlockSpec(memory_space=pltpu.HBM)] * 4,
+        out_specs=(pl.BlockSpec(memory_space=pltpu.VMEM), pl.BlockSpec(memory_space=pltpu.VMEM)),
         scratch_shapes=[
             pltpu.VMEM((chunks, depth, width), jnp.bfloat16),
+            pltpu.VMEM((per_dev, depth), jnp.bfloat16),
+            pltpu.VMEM((SLOT, depth), jnp.bfloat16),
             pltpu.VMEM((nrows, depth), jnp.bfloat16),
             pltpu.VMEM((TOP, share), jnp.int32),
             pltpu.VMEM((DEV_TOP, share), jnp.int32),
-            pltpu.VMEM((ndev, chunks, 4, width), jnp.int32),
-            pltpu.VMEM((ndev, chunks, 4, width), jnp.int32),
+            pltpu.VMEM((pairs, chunks, 4, width), jnp.int32),
             pltpu.VMEM((1, 2 * padded), jnp.float32),
             pltpu.VMEM((everyone, 1, 2 * padded), jnp.float32),
             pltpu.VMEM((1, 128), jnp.float32),
             pltpu.VMEM((everyone, 1, 128), jnp.float32),
             pltpu.VMEM((nrows, 128), jnp.float32),
             dma((chunks,)),
-            dma((2,)),
-            dma((ndev,)),
-            dma((ndev,)),
-            dma((ndev,)),
-            dma((ndev,)),
-            dma((ndev,)),
-            dma((ndev,)),
+            dma((3,)),
+            dma((pairs,)),
+            dma((pairs,)),
+            dma((pairs,)),
+            dma((pairs,)),
+            dma((2 * pairs,)),
+            dma((2 * pairs,)),
+            dma((pairs,)),
+            dma((pairs, chunks)),
+            dma((pairs,)),
+            dma((pairs,)),
             dma,
             dma,
             dma,
             dma,
         ],
         compiler_params=pltpu.CompilerParams(
-            collective_id=0, has_side_effects=True, vmem_limit_bytes=60 * 1024 * 1024
+            collective_id=0, has_side_effects=True, vmem_limit_bytes=VMEM - share * ndev * 16 - 10747904
         ),
         name="route",
-    )(tokens, router, device_pick, expert_pick)
+    )(tokens, router.T, device_pick, expert_pick)
+    gates, device_max, balance = pl.pallas_call(
+        functools.partial(decode, (ndev, share, width, chunks)),
+        out_shape=(
+            jax.ShapeDtypeStruct((TOP, share * ndev), jnp.float32),
+            jax.ShapeDtypeStruct((1, share * ndev), jnp.float32),
+            jax.ShapeDtypeStruct((3,), jnp.float32),
+        ),
+        in_specs=[pl.BlockSpec(memory_space=pltpu.VMEM)] * 2,
+        out_specs=(
+            pl.BlockSpec(memory_space=pl.ANY),
+            pl.BlockSpec(memory_space=pl.ANY),
+            pl.BlockSpec(memory_space=pltpu.SMEM),
+        ),
+        scratch_shapes=[
+            pltpu.VMEM((TOP, share * ndev), jnp.float32),
+            pltpu.VMEM((1, share * ndev), jnp.float32),
+            dma((2, ndev)),
+        ],
+        compiler_params=pltpu.CompilerParams(vmem_limit_bytes=8 * 1024 * 1024),
+        name="decode",
+    )(messages, sums)
     return gates, device_max, balance
 
 

time: 44.7 us -> 42.9 us (0.960)
  local copies, waits for them, and re-layouts: 6.5 us -> 0.88 us
  Pallas kernels: 37.3 us -> 41.2 us
    unnamed x3 -> x2, local copies, waits for them, and re-layouts: 4.96 us -> 0.88 us
    pallas_call x0 -> x1, Pallas kernels: none -> 2.38 us  [local(): pl.pallas_call(functools.partial(decode, (ndev, share, width, chunks)), o...]
    pad x1 -> x0, local copies, waits for them, and re-layouts: 1.54 us -> none  [local(): router = jnp.pad(router.T, ((0, SLOT - per_dev), (0, 0)))]
    pallas_call x1, Pallas kernels: 37.3 us -> 38.8 us  [local(): pl.pallas_call(functools.partial(kernel, (ndp, ndev, per_dev, width, chun...]
where the time goes in v2:
time: 42.9 us; the launch traced here: 42.7 us
  Pallas kernels  41.2 us (96%)
  local copies, waits for them, and re-layouts  0.88 us (2%)
  between operations  0.65 us (2%)
    pallas_call x1, Pallas kernels, local(): pl.pallas_call(functools.partial(kernel, (ndp, ndev, per_dev, width, chun...  38.8 us
    pallas_call x1, Pallas kernels, local(): pl.pallas_call(functools.partial(decode, (ndev, share, width, chunks)), o...  2.38 us
    unnamed x2, local copies, waits for them, and re-layouts  0.88 us

profile of v2, /device:TPU:0, one launch (start us, length us, event | category | flops | bytes accessed | tf_op | source)
XLA Modules:
  0.0 42.7 jit_solution(7168899437695875106)
XLA Ops:
  0.6 0.0 copy-start
  0.6 0.9 %copy-done = bf16[5120,5]{0,1:T(8,128)(2,1)S(1)} copy-done((bf16[5120,5]{0,1:T(8,128)(2,1)S(1)}, bf16[5120,5]{0,1:T(8,128)(2,1)}, u32[]{:S(2)}) %copy-start) | copy-done | bytes 51224
  1.5 38.8 %route.1 = (s32[8,8,4,512]{3,2,1,0:T(4,128)S(1)}, f32[1,128]{1,0:T(1,128)S(1)}) custom-call(bf16[5120,4096]{1,0:T(8,128)(2,1)} %tokens.1, bf16[5,5120]{1,0:T(8,128)(2,1)S(1)} %bitcast.1, s32[3,32768]{1,0:T(4,128)} %device_pick.1, s32[6,32768]{1,0:T(8,128)} %expert_pick.1), custom_call_target="tpu_custom_call" | custom-call | tf_op jit(solution)/shard_map/route/pallas_call | solution.py:337
  40.3 2.4 %decode.1 = (f32[6,32768]{1,0:T(8,128)}, f32[1,32768]{1,0:T(1,128)}, f32[3]{0:T(128)}) custom-call(s32[8,8,4,512]{3,2,1,0:T(4,128)S(1)} %get-tuple-element.5.recv_msg, f32[1,128]{1,0:T(1,128)S(1)} %get-tuple-element.6.sums), custom_call_target="tpu_custom_call" | custom-call | tf_op jit(solution)/shard_map/decode/pallas_call | solution.py:380
Async XLA Ops:
  0.6 0.9 %copy-start = (bf16[5120,5]{0,1:T(8,128)(2,1)S(1)}, bf16[5120,5]{0,1:T(8,128)(2,1)}, u32[]{:S(2)}) copy-start(bf16[5120,5]{0,1:T(8,128)(2,1)} %param.5) | copy-start | bytes 153604
